TPU v7x, 32 devices: a whole 2x2x4 slice. The times are simulated.
32 devices in a mesh: dp: 2 (over core), fsdp: 16 (over z, y, x).
Axes of the slice: x: 2, y: 2, z: 4, core: 2. Of those that a mesh axis runs over, the one named last changes fastest.
Arguments:
- tokens: bfloat16 [8192, 4096], P(('dp', 'fsdp')), may hold values from -6 to 6
- block_codes: bfloat16 [256, 128, 128], P('fsdp'), may hold values from -4 to 4
- scales: float32 [256], P('fsdp'), may hold values from 0.008 to 0.03
- counts: int32 [16], replicated, may hold values from 0 to 16, as said below
- cotangent: bfloat16 [8192, 512], P(('dp', 'fsdp')), may hold values from -6 to 6
Outputs:
- projected: bfloat16 [8192, 512], P(('dp', 'fsdp'))
- token_grad: bfloat16 [8192, 4096], P(('dp', 'fsdp'))
- block_grad: bfloat16 [256, 128, 128], P('fsdp')
Inputs may be any that keep to these rules, and one draw needn't show every extreme that they name: counts sum to 128; each is at most 16, and some owner has exactly 16 and some none; slots past an owner's count hold values that are not used.
All inputs are finite; a program needn't handle non-finite values.
Results may differ from a plain program's by a relative error of at most 0.009.
Values may be sent and summed in bfloat16 or wider, within the bound.
A program may use at most 128 MiB of HBM per device.

v0:
```python
import math

import jax
import jax.numpy as jnp
from jax import lax
from jax.sharding import PartitionSpec as P


def block_index(counts, owners_total, block_count, most_slots):
    run_ends = jnp.cumsum(counts)
    offsets = run_ends - counts
    block_ids = jnp.arange(block_count, dtype=jnp.int32)
    owners = jnp.sum((run_ends[None, :] <= block_ids[:, None]).astype(jnp.int32), axis=1)
    matched = owners[:, None] == jnp.arange(owners_total, dtype=jnp.int32)[None, :]
    run_start = jnp.sum(jnp.where(matched, offsets[None, :], 0), axis=1)
    source_ids = owners * most_slots + block_ids - run_start
    return (offsets, source_ids)


def body(tokens, block_codes, scales, counts, cotangent):
    owners_total = lax.axis_size("fsdp")
    most_slots = block_codes.shape[0]
    tile_size = block_codes.shape[1]
    width = tokens.shape[1]
    key_width = cotangent.shape[1]
    row_tiles = width // tile_size
    col_tiles = key_width // tile_size
    block_count = row_tiles * col_tiles
    total_tokens = tokens.shape[0] * lax.axis_size("dp") * owners_total
    loss_scale = 1.0 / math.sqrt(total_tokens)
    offsets, source_ids = block_index(counts, owners_total, block_count, most_slots)
    own_blocks = (block_codes.astype(jnp.float32) * scales[:, None, None]).astype(jnp.bfloat16)
    all_blocks_held = lax.all_gather(own_blocks, "fsdp", axis=0, tiled=True)
    blocks = jnp.take(all_blocks_held, source_ids, axis=0)
    weight = (
        blocks.reshape(row_tiles, col_tiles, tile_size, tile_size)
        .transpose(0, 2, 1, 3)
        .reshape(width, key_width)
    )
    projected = jnp.dot(tokens, weight, preferred_element_type=jnp.float32).astype(jnp.bfloat16)
    token_grad = lax.dot_general(
        cotangent, weight, (((1,), (1,)), ((), ())), preferred_element_type=jnp.float32
    ).astype(jnp.bfloat16)
    local_grad = (
        lax.dot_general(
            tokens, cotangent, (((0,), (0,)), ((), ())), preferred_element_type=jnp.float32
        )
        * loss_scale
    )
    grad_blocks = (
        local_grad.reshape(row_tiles, tile_size, col_tiles, tile_size)
        .transpose(0, 2, 1, 3)
        .reshape(block_count, tile_size, tile_size)
    )
    evened = lax.psum_scatter(grad_blocks, "fsdp", scatter_dimension=0, tiled=True)
    evened = lax.psum(evened.astype(jnp.bfloat16), "dp").astype(jnp.float32)
    finished = lax.all_gather(evened.astype(jnp.bfloat16), "fsdp", axis=0, tiled=True)
    my_index = lax.axis_index("fsdp")
    is_mine = jnp.arange(owners_total, dtype=jnp.int32) == my_index
    my_start = jnp.sum(jnp.where(is_mine, offsets, 0))
    my_count = jnp.sum(jnp.where(is_mine, counts, 0))
    within = jnp.arange(most_slots, dtype=jnp.int32)
    wanted = my_start + within
    picked = jnp.take(finished, jnp.clip(wanted, 0, block_count - 1), axis=0)
    block_grad = jnp.where((within < my_count)[:, None, None], picked, jnp.zeros_like(picked))
    return (projected, token_grad, block_grad)


def solution(mesh):
    return jax.shard_map(
        body,
        mesh=mesh,
        in_specs=(
            P(("dp", "fsdp"), None),
            P("fsdp", None, None),
            P("fsdp"),
            P(),
            P(("dp", "fsdp"), None),
        ),
        out_specs=(P(("dp", "fsdp"), None), P(("dp", "fsdp"), None), P("fsdp", None, None)),
        check_vma=False,
    )
```

profile of v0, /device:TPU:0, one launch (start us, length us, event | category | flops | bytes accessed | tf_op | source)
XLA Modules:
  0.0 439.9 jit_solution(7048292042617960575)
XLA Ops:
  7.2 1.5 copy-done
  8.8 5.5 %convolution_multiply_fusion = f32[4096,512]{1,0:T(8,128)} fusion(bf16[256,4096]{1,0:T(8,128)(2,1)S(1)} %copy-done, bf16[256,512]{1,0:T(8,128)(2,1)} %param.9), kind=kOutput, calls=%fused_computation.2 | convolution fusion | flops 1075838976 | bytes 10747904 | tf_op jit(solution)/shard_map/dot_general | solution.py:45
  14.2 9.9 %reshape.119 = f32[32,128,4,128]{3,2,1,0:T(4,128)} reshape(f32[4096,512]{1,0:T(8,128)} %convolution_multiply_fusion) | data formatting | bytes 16777216 | tf_op jit(solution)/shard_map/reshape | solution.py:51
  24.1 7.9 %copy.33 = f32[32,128,4,128]{3,1,2,0:T(8,128)} copy(f32[32,128,4,128]{3,2,1,0:T(4,128)} %reshape.119) | data formatting | bytes 16777216 | tf_op jit(solution)/shard_map/reshape | solution.py:51
  32.0 0.0 all-reduce.2.cloned.1.call-start
  32.1 180.7 %reduce-scatter.2.cloned.1.call-done = f32[8,128,128]{2,1,0:T(8,128)} async-done(((f32[128,128,128]{2,1,0:T(8,128)}), f32[8,128,128]{2,1,0:T(8,128)}) %reduce-scatter.2.cloned.1.call-update) | async-done | bytes 524304 | tf_op jit(solution)/shard_map/reduce_scatter | solution.py:55
  212.7 1.8 convert_element_type.33
  214.6 1.0 multiply_convert_fusion
  215.7 20.7 %all-reduce.2.cloned.1.call-done = bf16[8,128,128]{2,1,0:T(8,128)(2,1)} async-done(((bf16[8,128,128]{2,1,0:T(8,128)(2,1)}), bf16[8,128,128]{2,1,0:T(8,128)(2,1)}) %all-reduce.2.cloned.1.call-update) | async-done | bytes 262160 | tf_op jit(solution)/shard_map/psum | solution.py:56
  236.3 0.1 copy.29
  236.5 0.1 reduce
  236.6 0.1 convert_reduce_fusion
  236.7 0.6 fusion.13
  237.3 0.1 select_reduce_fusion
  237.4 0.1 reduce_sum.42
  237.5 0.1 copy.31
  237.6 0.1 mul.38
  237.7 0.1 copy.30
  237.8 0.7 fusion.15
  238.4 1.3 compare_and_fusion
  239.8 113.4 %all-gather.3.cloned.1.call-done = bf16[256,128,128]{2,1,0:T(8,128)(2,1)} async-done(((bf16[16,128,128]{2,1,0:T(8,128)(2,1)}), bf16[256,128,128]{2,1,0:T(8,128)(2,1)}) %all-gather.3.cloned.1.call-update) | async-done | bytes 8388624 | tf_op jit(solution)/shard_map/all_gather | solution.py:33
  353.2 6.4 %gather_fusion = bf16[128,128,128]{2,1,0:T(8,128)(2,1)} fusion(bf16[256,128,128]{2,1,0:T(8,128)(2,1)} %all-gather.3.cloned.1.call-done, s32[1024]{0:T(1024)S(1)} %pad_clamp_fusion.1), kind=kCustom, calls=%fused_computation | custom fusion | bytes 8389120 | tf_op jit(solution)/shard_map/jit(_take)/gather | solution.py:34
  359.6 7.9 %copy.32 = bf16[32,4,128,128]{2,0,3,1:T(8,128)(2,1)} copy(bf16[32,4,128,128]{3,2,1,0:T(8,128)(2,1)} %bitcast.40) | data formatting | bytes 8388608 | tf_op jit(solution)/shard_map/jit(_take)/gather | solution.py:34
  367.6 2.7 broadcast_select_fusion
  370.2 1.9 copy-done.1
  372.2 1.5 fusion.9
  373.7 0.8 copy.34
  374.5 8.0 %fusion = bf16[256,4096]{0,1:T(8,128)(2,1)} fusion(bf16[256,512]{1,0:T(8,128)(2,1)S(1)} %copy-done.3, bf16[64,8,32,128]{3,2,1,0:T(8,128)(2,1)} %bitcast.42), kind=kOutput, calls=%fused_computation.4 | convolution fusion | flops 1074790400 | bytes 6553600 | tf_op jit(solution)/shard_map/dot_general | solution.py:41
  382.5 4.1 copy.35
  386.6 43.1 %all-gather.5.cloned.1.call-done = bf16[128,128,128]{2,1,0:T(8,128)(2,1)} async-done(((bf16[8,128,128]{2,1,0:T(8,128)(2,1)}), bf16[128,128,128]{2,1,0:T(8,128)(2,1)}) %all-gather.5.cloned.1.call-update) | async-done | bytes 4194320 | tf_op jit(solution)/shard_map/all_gather | solution.py:57
  429.6 2.8 gather_fusion.1
  432.5 0.9 select_select_fusion
  (23 shorter events, 0.3 us)
Async XLA Ops:
  7.2 1.6 copy-start
  7.2 205.6 %reduce-scatter.2.cloned.1.call-start = ((), (), s32[]{:S(2)}) async-start(), calls=%async_computation.2 | async-start | bytes 8912896 | tf_op jit(solution)/shard_map/reduce_scatter | solution.py:55
  32.0 182.6 %copy-start.2 = (bf16[16,128,128]{2,1,0:T(8,128)(2,1)S(1)}, bf16[16,128,128]{2,1,0:T(8,128)(2,1)}, u32[]{:S(2)}) copy-start(bf16[16,128,128]{2,1,0:T(8,128)(2,1)} %param.6) | copy-start | bytes 1572868
  32.0 182.6 %copy-start.5 = (f32[16]{0:T(128)S(1)}, f32[16]{0:T(128)}, u32[]{:S(2)}) copy-start(f32[16]{0:T(128)} %param.7) | copy-start | bytes 196
  32.0 204.4 %copy-start.4 = (s32[16]{0:T(128)S(1)}, s32[16]{0:T(128)}, u32[]{:S(2)}) copy-start(s32[16]{0:T(128)} %param.8) | copy-start | bytes 196
  32.0 204.3 %all-reduce.2.cloned.1.call-start = ((), (), s32[]{:S(2)}) async-start(), calls=%async_computation.3 | async-start | bytes 524288 | tf_op jit(solution)/shard_map/psum | solution.py:56
  214.5 138.7 %all-gather.3.cloned.1.call-start = ((), (), s32[]{:S(2)}) async-start(), calls=%async_computation.1 | async-start | bytes 8912896 | tf_op jit(solution)/shard_map/all_gather | solution.py:33
  215.6 214.0 %all-gather.5.cloned.1.call-start = ((), (), s32[]{:S(2)}) async-start(), calls=%async_computation.4 | async-start | bytes 4456448 | tf_op jit(solution)/shard_map/all_gather | solution.py:57
  370.2 1.9 copy-start.1
  372.2 2.4 copy-start.3
Sparse Core Ops, SparseCore 0:
  32.1 180.5 reduce-scatter.1
  215.6 20.6 all-reduce.1
  239.7 113.4 all-gather.2
  355.8 73.7 all-gather.4
where the time goes:
time: 441 us; the launch traced here: 440 us
  waiting for transfers between devices  358 us (81%)
  local copies, waits for them, and re-layouts  43.8 us (10%)
  matrix products  14.9 us (3%)
  between operations  13.9 us (3%)
  other arithmetic  9.34 us (2%)
    reduce_scatter x1, waiting for transfers between devices, body(): lax.psum_scatter(grad_blocks, 'fsdp', scatter_dimension=0, tiled=True)  181 us
    all_gather x1, waiting for transfers between devices, body(): all_blocks_held = lax.all_gather(own_blocks, 'fsdp', axis=0, tiled=True)  113 us
    all_gather x1, waiting for transfers between devices, body(): lax.all_gather(evened.astype(jnp.bfloat16), 'fsdp', axis=0, tiled=True)  43.1 us
    psum x1, waiting for transfers between devices, body(): evened = lax.psum(evened.astype(jnp.bfloat16), 'dp').astype(jnp.float32)  20.7 us
    reshape x2, local copies, waits for them, and re-layouts, body(): local_grad.reshape(row_tiles, tile_size, col_tiles, tile_size)  17.8 us
    gather x2, local copies, waits for them, and re-layouts, body(): blocks = jnp.take(all_blocks_held, source_ids, axis=0)  14.4 us
  transfers between devices with their start and end apart: 4, of which 4 were waited for; matrix products, arithmetic and copies ran while one was open for 8% of the time, Pallas kernels for 0%

commit v1 on v0

v1 whole, which is shorter than its diff:
```python
import functools
import math

import jax
import jax.numpy as jnp
from jax import lax
from jax.experimental import pallas as pl
from jax.experimental.pallas import tpu as pltpu
from jax.sharding import PartitionSpec as P

MESH = pl.DeviceIdType.MESH
F32 = jnp.float32
BF16 = jnp.bfloat16


def block_index(counts, owners_total, block_count, most_slots):
    run_ends = jnp.cumsum(counts)
    offsets = run_ends - counts
    block_ids = jnp.arange(block_count, dtype=jnp.int32)
    owners = jnp.sum((run_ends[None, :] <= block_ids[:, None]).astype(jnp.int32), axis=1)
    matched = owners[:, None] == jnp.arange(owners_total, dtype=jnp.int32)[None, :]
    run_start = jnp.sum(jnp.where(matched, offsets[None, :], 0), axis=1)
    source_ids = owners * most_slots + block_ids - run_start
    return (offsets, source_ids)


def grad_kernel(scale, tile, tok_ref, cot_ref, out_ref):
    half = tile // 2
    part = lax.dot_general(
        tok_ref[...], cot_ref[...], (((0,), (0,)), ((), ())), preferred_element_type=F32
    )
    part = (part * scale).astype(BF16)
    rows, cols = part.shape[0] // tile, part.shape[1] // tile
    for r in range(rows):
        for c in range(cols):
            for h in range(2):
                top = r * tile + h * half
                out_ref[h, r * cols + c] = part[top : top + half, c * tile : (c + 1) * tile]


def weight_kernel(tile, chunks, ids_ref, tok_ref, cot_ref, held_ref, proj_ref, tg_ref, w_ref, acc_ref, sems):
    step = pl.program_id(0)
    depth = w_ref.shape[1]
    cols = w_ref.shape[2] // tile
    rows = depth // tile

    @pl.when(step == 0)
    def _():
        def fetch(g, _):
            for r in range(rows):
                for c in range(cols):
                    b = (g * rows + r) * cols + c
                    pltpu.make_async_copy(
                        held_ref.at[ids_ref[b]],
                        w_ref.at[g, pl.ds(r * tile, tile), pl.ds(c * tile, tile)],
                        sems.at[g],
                    ).start()
            return 0

        lax.fori_loop(0, chunks, fetch, 0)
        acc_ref[...] = jnp.zeros_like(acc_ref)

    pltpu.make_async_copy(w_ref.at[step], w_ref.at[step], sems.at[step]).wait()
    weight = w_ref[step]
    acc_ref[...] += jnp.dot(tok_ref[...], weight, preferred_element_type=F32)
    tg_ref[...] = lax.dot_general(
        cot_ref[...], weight, (((1,), (1,)), ((), ())), preferred_element_type=F32
    ).astype(BF16)

    @pl.when(step == chunks - 1)
    def _():
        proj_ref[...] = acc_ref[...].astype(BF16)


def comm_kernel(
    outer, inner, idx_ref, own_ref, g_ref, held_ref, out_ref,
    pair_buf, sb, ra1, rb1, ta, tb, ra2, rb2,
    local_sem, pair_sems, gi_send, gi_recv, go_send, go_recv, fi_send, fi_recv, fo_send, fo_recv,
    ri_send, ri_recv, ro_send, ro_recv, out_sems,
):
    core = lax.axis_index("dp")
    other = 1 - core
    me = lax.axis_index("fsdp")
    o = me // inner
    i = me % inner
    slots, tile = own_ref.shape[0], own_ref.shape[1]
    half, q = tile // 2, tile // 4

    def rows(c, p):
        return pl.ds(pl.multiple_of(c * half + p * q, q), q)

    partner = (other, me)

    def mate_in(k):
        return (core, o * inner + (i + k) % inner)

    def mate_out(k):
        return (core, ((o + k) % outer) * inner + i)

    def remote(src, dst, send, recv, device):
        return pltpu.make_async_remote_copy(
            src_ref=src, dst_ref=dst, send_sem=send, recv_sem=recv,
            device_id=device, device_id_type=MESH,
        )

    barrier = pltpu.get_barrier_semaphore()
    peers = [partner] + [mate_in(k) for k in range(1, inner)] + [mate_out(k) for k in range(1, outer)]
    for peer in peers:
        pl.semaphore_signal(barrier, inc=1, device_id=peer, device_id_type=MESH)
    pl.semaphore_wait(barrier, len(peers))

    started = []

    def go(copy):
        copy.start()
        started.append(copy)
        return copy

    pair = remote(g_ref.at[other], pair_buf, pair_sems.at[0], pair_sems.at[1], partner)
    pair.start()
    a1 = [
        go(remote(own_ref.at[:, rows(core, 0)], held_ref.at[o, i, :, rows(core, 0)],
                  gi_send.at[0, k], gi_recv.at[0, k], mate_in(k)))
        for k in range(1, inner)
    ]
    b1 = [
        go(remote(own_ref.at[:, rows(core, 1)], held_ref.at[o, i, :, rows(core, 1)],
                  go_send.at[0, k], go_recv.at[0, k], mate_out(k)))
        for k in range(1, outer)
    ]
    mine = pltpu.make_async_copy(own_ref, held_ref.at[o, i], local_sem)
    mine.start()

    pair.wait_recv()

    def build(s, _):
        oo, ii, j = s // (inner * slots), (s // slots) % inner, s % slots
        b = idx_ref[s]
        total = g_ref[core, b].astype(F32) + pair_buf[b].astype(F32)
        total = total.astype(BF16)
        sb[0, oo, ii, j] = total[:q]
        sb[1, oo, ii, j] = total[q:]
        return 0

    lax.fori_loop(0, outer * inner * slots, build, 0, unroll=4)

    ga1 = [
        go(remote(sb.at[0, (o + k) % outer], ra1.at[k], ro_send.at[0, k], ro_recv.at[0, k], mate_out(k)))
        for k in range(1, outer)
    ]
    gb1 = [
        go(remote(sb.at[1, :, (i + k) % inner], rb1.at[k], ri_send.at[0, k], ri_recv.at[0, k], mate_in(k)))
        for k in range(1, inner)
    ]

    forwards = []

    def forward(place, send, recv):
        copy = remote(place, place, send, recv, partner)
        copy.start()
        forwards.append(copy)

    mine.wait()
    for k, copy in enumerate(a1, 1):
        copy.wait_recv()
    a2 = [
        go(remote(held_ref.at[o, :, :, rows(core, 0)], held_ref.at[o, :, :, rows(core, 0)],
                  go_send.at[1, k], go_recv.at[1, k], mate_out(k)))
        for k in range(1, outer)
    ]
    for k, copy in enumerate(b1, 1):
        copy.wait_recv()
    b2 = [
        go(remote(held_ref.at[:, i, :, rows(core, 1)], held_ref.at[:, i, :, rows(core, 1)],
                  gi_send.at[1, k], gi_recv.at[1, k], mate_in(k)))
        for k in range(1, inner)
    ]
    for k in range(1, inner):
        forward(held_ref.at[o, (i - k + inner) % inner, :, rows(core, 0)], fi_send.at[0, k], fi_recv.at[0, k])
    for k in range(1, outer):
        forward(held_ref.at[(o - k + outer) % outer, i, :, rows(core, 1)], fo_send.at[0, k], fo_recv.at[0, k])

    for copy in ga1:
        copy.wait_recv()

    def sum_a(s, _):
        ii, j = s // slots, s % slots
        total = sb[0, o, ii, j].astype(F32)
        for k in range(1, outer):
            total += ra1[k, ii, j].astype(F32)
        ta[ii, j] = total.astype(BF16)
        return 0

    lax.fori_loop(0, inner * slots, sum_a, 0)
    ga2 = [
        go(remote(ta.at[(i + k) % inner], ra2.at[k], ri_send.at[1, k], ri_recv.at[1, k], mate_in(k)))
        for k in range(1, inner)
    ]
    for copy in gb1:
        copy.wait_recv()

    def sum_b(s, _):
        oo, j = s // slots, s % slots
        total = sb[1, oo, i, j].astype(F32)
        for k in range(1, inner):
            total += rb1[k, oo, j].astype(F32)
        tb[oo, j] = total.astype(BF16)
        return 0

    lax.fori_loop(0, outer * slots, sum_b, 0)
    gb2 = [
        go(remote(tb.at[(o + k) % outer], rb2.at[k], ro_send.at[1, k], ro_recv.at[1, k], mate_out(k)))
        for k in range(1, outer)
    ]

    for k, copy in enumerate(a2, 1):
        copy.wait_recv()
        forward(held_ref.at[(o - k + outer) % outer, :, :, rows(core, 0)], fo_send.at[1, k], fo_recv.at[1, k])
    for k, copy in enumerate(b2, 1):
        copy.wait_recv()
        forward(held_ref.at[:, (i - k + inner) % inner, :, rows(core, 1)], fi_send.at[1, k], fi_recv.at[1, k])

    for copy in ga2 + gb2:
        copy.wait_recv()

    def last(j, _):
        total = ta[i, j].astype(F32)
        for k in range(1, inner):
            total += ra2[k, j].astype(F32)
        out_ref[j, rows(core, 0)] = total.astype(BF16)
        total = tb[o, j].astype(F32)
        for k in range(1, outer):
            total += rb2[k, j].astype(F32)
        out_ref[j, rows(core, 1)] = total.astype(BF16)
        return 0

    lax.fori_loop(0, slots, last, 0)
    place = out_ref.at[:, pl.ds(pl.multiple_of(core * half, half), half)]
    swap = remote(place, place, out_sems.at[0], out_sems.at[1], partner)
    swap.start()
    for copy in started:
        copy.wait_send()
    pair.wait_send()
    for copy in forwards:
        copy.wait()
    swap.wait()


def body(tokens, block_codes, scales, counts, cotangent):
    owners_total = lax.axis_size("fsdp")
    most_slots, tile = block_codes.shape[0], block_codes.shape[1]
    local_tokens, width = tokens.shape
    key_width = cotangent.shape[1]
    row_tiles, col_tiles = width // tile, key_width // tile
    block_count = row_tiles * col_tiles
    total_tokens = local_tokens * lax.axis_size("dp") * owners_total
    loss_scale = 1.0 / math.sqrt(total_tokens)
    inner = 4 if owners_total % 4 == 0 else 1
    outer = owners_total // inner
    half, q = tile // 2, tile // 4
    all_slots = owners_total * most_slots
    offsets, source_ids = block_index(counts, owners_total, block_count, most_slots)
    within = jnp.arange(most_slots, dtype=jnp.int32)
    wanted = jnp.clip(offsets[:, None] + within[None, :], 0, block_count - 1).reshape(all_slots)
    own_blocks = (block_codes.astype(F32) * scales[:, None, None]).astype(BF16)

    chunks = 8
    depth = width // chunks
    grads = pl.pallas_call(
        functools.partial(grad_kernel, loss_scale, tile),
        grid=(chunks,),
        in_specs=[
            pl.BlockSpec((local_tokens, depth), lambda g: (0, g)),
            pl.BlockSpec((local_tokens, key_width), lambda g: (0, 0)),
        ],
        out_specs=pl.BlockSpec((2, block_count // chunks, half, tile), lambda g: (0, g, 0, 0)),
        out_shape=jax.ShapeDtypeStruct((2, block_count, half, tile), BF16),
    )(tokens, cotangent)

    dma = pltpu.SemaphoreType.DMA
    vmem = pl.BlockSpec(memory_space=pltpu.VMEM)
    held, picked = pl.pallas_call(
        functools.partial(comm_kernel, outer, inner),
        in_specs=[pl.BlockSpec(memory_space=pltpu.SMEM), vmem, vmem],
        out_specs=[pl.BlockSpec(memory_space=pl.ANY), vmem],
        out_shape=[
            jax.ShapeDtypeStruct((outer, inner, most_slots, tile, tile), BF16),
            jax.ShapeDtypeStruct((most_slots, tile, tile), BF16),
        ],
        scratch_shapes=[
            pltpu.VMEM((block_count, half, tile), BF16),
            pltpu.VMEM((2, outer, inner, most_slots, q, tile), BF16),
            pltpu.VMEM((outer, inner, most_slots, q, tile), BF16),
            pltpu.VMEM((inner, outer, most_slots, q, tile), BF16),
            pltpu.VMEM((inner, most_slots, q, tile), BF16),
            pltpu.VMEM((outer, most_slots, q, tile), BF16),
            pltpu.VMEM((inner, most_slots, q, tile), BF16),
            pltpu.VMEM((outer, most_slots, q, tile), BF16),
            dma,
            dma((2,)),
            dma((2, inner)), dma((2, inner)), dma((2, outer)), dma((2, outer)),
            dma((2, inner)), dma((2, inner)), dma((2, outer)), dma((2, outer)),
            dma((2, inner)), dma((2, inner)), dma((2, outer)), dma((2, outer)),
            dma((2,)),
        ],
        compiler_params=pltpu.CompilerParams(
            collective_id=0, has_side_effects=True, vmem_limit_bytes=48 * 1024 * 1024
        ),
    )(wanted, own_blocks, grads)

    held = held.reshape(all_slots, tile, tile)
    projected, token_grad = pl.pallas_call(
        functools.partial(weight_kernel, tile, chunks),
        grid_spec=pltpu.PrefetchScalarGridSpec(
            num_scalar_prefetch=1,
            grid=(chunks,),
            in_specs=[
                pl.BlockSpec((local_tokens, depth), lambda g, ids: (0, g)),
                pl.BlockSpec((local_tokens, key_width), lambda g, ids: (0, 0)),
                pl.BlockSpec(memory_space=pl.ANY),
            ],
            out_specs=[
                pl.BlockSpec((local_tokens, key_width), lambda g, ids: (0, 0)),
                pl.BlockSpec((local_tokens, depth), lambda g, ids: (0, g)),
            ],
            scratch_shapes=[
                pltpu.VMEM((chunks, depth, key_width), BF16),
                pltpu.VMEM((local_tokens, key_width), F32),
                dma((chunks,)),
            ],
        ),
        out_shape=[
            jax.ShapeDtypeStruct((local_tokens, key_width), BF16),
            jax.ShapeDtypeStruct((local_tokens, width), BF16),
        ],
    )(source_ids, tokens, cotangent, held)

    is_mine = jnp.arange(owners_total, dtype=jnp.int32) == lax.axis_index("fsdp")
    my_count = jnp.sum(jnp.where(is_mine, counts, 0))
    block_grad = jnp.where((within < my_count)[:, None, None], picked, jnp.zeros_like(picked))
    return (projected, token_grad, block_grad)


def solution(mesh):
    return jax.shard_map(
        body,
        mesh=mesh,
        in_specs=(
            P(("dp", "fsdp"), None),
            P("fsdp", None, None),
            P("fsdp"),
            P(),
            P(("dp", "fsdp"), None),
        ),
        out_specs=(P(("dp", "fsdp"), None), P(("dp", "fsdp"), None), P("fsdp", None, None)),
        check_vma=False,
    )
```

time: 441 us -> 146 us (0.33)
  waiting for transfers between devices: 358 us -> 0 us
  Pallas kernels: 0 us -> 137 us
  local copies, waits for them, and re-layouts: 43.8 us -> 3 us
  matrix products: 14.9 us -> 0 us
  between operations: 13.9 us -> 0.67 us
    reduce_scatter x1 -> x0, waiting for transfers between devices: 181 us -> none  [body(): lax.psum_scatter(grad_blocks, 'fsdp', scatter_dimension=0, tiled=True)]
    all_gather x2 -> x0, waiting for transfers between devices: 156 us -> none  [the longest x1 113 us: body(): all_blocks_held = lax.all_gather(own_blocks, 'fsdp', axis=0, tiled=True)]
    pallas_call x0 -> x3, Pallas kernels: none -> 137 us  [the longest x1 121 us: body(): pl.pallas_call(functools.partial(comm_kernel, outer, inner), in_specs=[pl...]
    psum x1 -> x0, waiting for transfers between devices: 20.7 us -> none  [body(): evened = lax.psum(evened.astype(jnp.bfloat16), 'dp').astype(jnp.float32)]
    reshape x2 -> x0, local copies, waits for them, and re-layouts: 17.8 us -> none  [body(): local_grad.reshape(row_tiles, tile_size, col_tiles, tile_size)]
    gather x3 -> x0, local copies, waits for them, and re-layouts: 17.2 us -> none  [the longest x2 14.4 us: body(): blocks = jnp.take(all_blocks_held, source_ids, axis=0)]
    dot_general x3 -> x0, matrix products: 14.9 us -> none  [the longest x1 7.96 us: body(): lax.dot_general(cotangent, weight, (((1,), (1,)), ((), ())), preferred_el...]
    unnamed x14 -> x2, local copies, waits for them, and re-layouts: 8.39 us -> 2.19 us
  transfers between devices with their start and end apart: 4 -> 0, of which waited for: 4 -> 0; matrix products, arithmetic and copies ran while one was open for 8% -> 0% of each run, Pallas kernels for 0% -> 0%
where the time goes in v1:
time: 146 us
  Pallas kernels  137 us (94%)
  other arithmetic  4.98 us (3%)
  local copies, waits for them, and re-layouts  3 us (2%)
    pallas_call x1, Pallas kernels, body(): pl.pallas_call(functools.partial(comm_kernel, outer, inner), in_specs=[pl...  121 us
    pallas_call x1, Pallas kernels, body(): pl.pallas_call(functools.partial(weight_kernel, tile, chunks), grid_spec=...  9.28 us
    pallas_call x1, Pallas kernels, body(): pl.pallas_call(functools.partial(grad_kernel, loss_scale, tile), grid=(ch...  7.3 us

profile of v1, /device:TPU:0, one launch (start us, length us, event | category | flops | bytes accessed | tf_op | source)
XLA Modules:
  0.0 145.8 jit_solution(15510233173077546647)
XLA Ops:
  0.6 0.7 copy.10
  1.4 0.1 reduce
  1.5 0.1 convert_reduce_fusion
  1.6 1.3 fusion
  2.9 0.1 select_reduce_fusion
  3.0 0.5 add_subtract_fusion.ids_ref
  3.5 0.6 iota_compare_fusion.2
  4.2 0.1 add_clamp_fusion
  4.2 0.1 min.12.idx_ref
  4.3 1.2 multiply_convert_fusion.own_ref
  5.5 7.3 %shard_map.76.g_ref = bf16[2,128,64,128]{3,2,1,0:T(8,128)(2,1)} custom-call(bf16[256,4096]{1,0:T(8,128)(2,1)} %tok_ref.3, bf16[256,512]{1,0:T(8,128)(2,1)} %cot_ref.3), custom_call_target="tpu_custom_call" | custom-call | tf_op jit(solution)/shard_map/pallas_call | solution.py:269
  12.8 0.0 copy-start
  12.9 2.2 %copy-done = bf16[2,128,64,128]{3,2,1,0:T(8,128)(2,1)S(1)} copy-done((bf16[2,128,64,128]{3,2,1,0:T(8,128)(2,1)S(1)}, bf16[2,128,64,128]{3,2,1,0:T(8,128)(2,1)}, u32[]{:S(2)}) %copy-start) | copy-done | bytes 4194328
  15.0 120.6 %shard_map.77 = (bf16[4,4,16,128,128]{4,3,2,1,0:T(8,128)(2,1)}, bf16[16,128,128]{2,1,0:T(8,128)(2,1)S(1)}) custom-call(s32[256]{0:T(256)S(1)} %min.12.idx_ref, bf16[16,128,128]{2,1,0:T(8,128)(2,1)S(1)} %multiply_convert_fusion.own_ref, bf16[2,128,64,128]{3,2,1,0:T(8,128)(2,1)S(1)} %copy-done), custom_call_target="tpu_custom_call" | custom-call | tf_op jit(solution)/shard_map/pallas_call | solution.py:282
  135.6 9.3 %shard_map.78 = (bf16[256,512]{1,0:T(8,128)(2,1)}, bf16[256,4096]{1,0:T(8,128)(2,1)}) custom-call(s32[128]{0:T(128)} %add_subtract_fusion.ids_ref, bf16[256,4096]{1,0:T(8,128)(2,1)} %tok_ref.3, bf16[256,512]{1,0:T(8,128)(2,1)} %cot_ref.3, bf16[256,128,128]{2,1,0:T(8,128)(2,1)} %bitcast.2), custom_call_target="tpu_custom_call" | custom-call | tf_op jit(solution)/shard_map/pallas_call | solution.py:312
  144.9 0.9 broadcast_select_fusion
  (1 shorter events, 0.0 us)
Async XLA Ops:
  12.8 2.2 %copy-start = (bf16[2,128,64,128]{3,2,1,0:T(8,128)(2,1)S(1)}, bf16[2,128,64,128]{3,2,1,0:T(8,128)(2,1)}, u32[]{:S(2)}) copy-start(bf16[2,128,64,128]{3,2,1,0:T(8,128)(2,1)} %shard_map.76.g_ref) | copy-start | bytes 12582916

commit v2 on v1

v2 whole, which is shorter than its diff:
```python
import functools
import math

import jax
import jax.numpy as jnp
from jax import lax
from jax.experimental import pallas as pl
from jax.experimental.pallas import tpu as pltpu
from jax.sharding import PartitionSpec as P

MESH = pl.DeviceIdType.MESH
F32 = jnp.float32
BF16 = jnp.bfloat16


def grad_kernel(scale, tile, tok_ref, cot_ref, out_ref):
    half = tile // 2
    part = lax.dot_general(
        tok_ref[...], cot_ref[...], (((0,), (0,)), ((), ())), preferred_element_type=F32
    )
    part = (part * scale).astype(BF16)
    rows, cols = part.shape[0] // tile, part.shape[1] // tile
    for r in range(rows):
        for c in range(cols):
            for h in range(2):
                top = r * tile + h * half
                out_ref[h, r * cols + c] = part[top : top + half, c * tile : (c + 1) * tile]


def weight_kernel(tile, chunks, owners, tok_ref, cot_ref, held_ref, proj_ref, tg_ref, w_ref, acc_ref, sems):
    step = pl.program_id(0)
    depth = w_ref.shape[1]
    cols = w_ref.shape[2] // tile
    rows = depth // tile

    @pl.when(step == 0)
    def _():
        def fetch(g, _):
            for r in range(rows):
                for c in range(cols):
                    b = (g * rows + r) * cols + c
                    pltpu.make_async_copy(
                        held_ref.at[b % owners, b // owners],
                        w_ref.at[g, pl.ds(r * tile, tile), pl.ds(c * tile, tile)],
                        sems.at[g],
                    ).start()
            return 0

        lax.fori_loop(0, chunks, fetch, 0)
        acc_ref[...] = jnp.zeros_like(acc_ref)

    pltpu.make_async_copy(w_ref.at[step], w_ref.at[step], sems.at[step]).wait()
    weight = w_ref[step]
    acc_ref[...] += jnp.dot(tok_ref[...], weight, preferred_element_type=F32)
    tg_ref[...] = lax.dot_general(
        cot_ref[...], weight, (((1,), (1,)), ((), ())), preferred_element_type=F32
    ).astype(BF16)

    @pl.when(step == chunks - 1)
    def _():
        proj_ref[...] = acc_ref[...].astype(BF16)


def comm_kernel(
    outer, inner, q0, counts_ref, scales_ref, codes_ref, g_ref, held_ref, out_ref,
    pair_buf, wsend, wrecv, stage, sb0, sb1, ra1, rb1, ta, tb, ra2, rb2, fin, gsend, grecv,
    local_sem, pair_sems, w_send, w_recv, x_send, x_recv, own_sems,
    gi_send, gi_recv, go_send, go_recv, fi_send, fi_recv, fo_send, fo_recv,
    ri_send, ri_recv, ro_send, ro_recv, out_sems,
):
    owners = outer * inner
    core = lax.axis_index("dp")
    other = 1 - core
    me = lax.axis_index("fsdp")
    o = me // inner
    i = me % inner
    slots, tile = codes_ref.shape[0], codes_ref.shape[1]
    even = stage.shape[0]
    half = tile // 2
    q1 = half - q0
    my_half = pl.ds(pl.multiple_of(core * half, half), half)
    parts = (pl.ds(0, q0), pl.ds(q0, q1))

    def rows(p):
        return pl.ds(pl.multiple_of(core * half + p * q0, q0), (q0, q1)[p])

    partner = (other, me)

    def mate_in(k):
        return (core, o * inner + (i + k) % inner)

    def mate_out(k):
        return (core, ((o + k) % outer) * inner + i)

    def mate(k):
        return (core, (me + k) % owners)

    def remote(src, dst, send, recv, device):
        return pltpu.make_async_remote_copy(
            src_ref=src, dst_ref=dst, send_sem=send, recv_sem=recv,
            device_id=device, device_id_type=MESH,
        )

    barrier = pltpu.get_barrier_semaphore()
    peers = [partner] + [mate(k) for k in range(1, owners)]
    for peer in peers:
        pl.semaphore_signal(barrier, inc=1, device_id=peer, device_id_type=MESH)
    pl.semaphore_wait(barrier, len(peers))

    started = []

    def go(copy):
        copy.start()
        started.append(copy)
        return copy

    pair = go(remote(g_ref.at[other], pair_buf, pair_sems.at[0], pair_sems.at[1], partner))

    offsets, ends, run, my_off, my_count = [], [], 0, 0, 0
    for d in range(owners):
        count = counts_ref[d]
        offsets.append(run)
        run = run + count
        ends.append(run)
        my_off = my_off + jnp.where(d < me, count, 0)
        my_count = my_count + jnp.where(d == me, count, 0)

    for k in range(owners):
        e = (me + k) % owners
        slot = jnp.minimum(lax.rem(e - my_off + even * owners, owners), slots - 1)
        block = (codes_ref[slot, my_half].astype(F32) * scales_ref[slot]).astype(BF16)
        if k == 0:
            wrecv[me] = block
        else:
            wsend[k] = block
    w_copies = [
        go(remote(wsend.at[k], wrecv.at[me], w_send.at[k], w_recv.at[k], mate(k)))
        for k in range(1, owners)
    ]

    pair.wait_recv()

    def build(s, _):
        oo, ii, m = s // (inner * even), (s // even) % inner, s % even
        b = m * owners + oo * inner + ii
        total = g_ref[core, b].astype(F32) + pair_buf[b].astype(F32)
        total = total.astype(BF16)
        sb0[oo, ii, m] = total[:q0]
        sb1[oo, ii, m] = total[q0:]
        return 0

    lax.fori_loop(0, owners * even, build, 0, unroll=4)

    ga1 = [
        go(remote(sb0.at[(o + k) % outer], ra1.at[k], ro_send.at[0, k], ro_recv.at[0, k], mate_out(k)))
        for k in range(1, outer)
    ]
    gb1 = [
        go(remote(sb1.at[:, (i + k) % inner], rb1.at[k], ri_send.at[0, k], ri_recv.at[0, k], mate_in(k)))
        for k in range(1, inner)
    ]

    for copy in w_copies:
        copy.wait_recv()
    for m in range(even):
        owner = 0
        for d in range(owners):
            owner = owner + jnp.where(ends[d] <= m * owners + me, 1, 0)
        stage[m] = wrecv[jnp.minimum(owner, owners - 1)]
    a1 = [
        go(remote(stage.at[:, parts[0]], held_ref.at[o, i, :, rows(0)],
                  gi_send.at[0, k], gi_recv.at[0, k], mate_in(k)))
        for k in range(1, inner)
    ]
    b1 = [
        go(remote(stage.at[:, parts[1]], held_ref.at[o, i, :, rows(1)],
                  go_send.at[0, k], go_recv.at[0, k], mate_out(k)))
        for k in range(1, outer)
    ]
    mine = pltpu.make_async_copy(stage, held_ref.at[o, i, :, my_half], local_sem)
    mine.start()
    forwards = []

    def forward(src, place, send, recv):
        copy = remote(src, place, send, recv, partner)
        copy.start()
        forwards.append(copy)

    forward(stage, held_ref.at[o, i, :, my_half], own_sems.at[0], own_sems.at[1])

    mine.wait()
    for copy in a1:
        copy.wait_recv()
    a2 = [
        go(remote(held_ref.at[o, :, :, rows(0)], held_ref.at[o, :, :, rows(0)],
                  go_send.at[1, k], go_recv.at[1, k], mate_out(k)))
        for k in range(1, outer)
    ]
    for copy in b1:
        copy.wait_recv()
    b2 = [
        go(remote(held_ref.at[:, i, :, rows(1)], held_ref.at[:, i, :, rows(1)],
                  gi_send.at[1, k], gi_recv.at[1, k], mate_in(k)))
        for k in range(1, inner)
    ]
    for k in range(1, inner):
        place = held_ref.at[o, (i - k + inner) % inner, :, rows(0)]
        forward(place, place, fi_send.at[0, k], fi_recv.at[0, k])
    for k in range(1, outer):
        place = held_ref.at[(o - k + outer) % outer, i, :, rows(1)]
        forward(place, place, fo_send.at[0, k], fo_recv.at[0, k])

    for copy in ga1:
        copy.wait_recv()

    def sum_a(s, _):
        ii, m = s // even, s % even
        total = sb0[o, ii, m].astype(F32)
        for k in range(1, outer):
            total += ra1[k, ii, m].astype(F32)
        ta[ii, m] = total.astype(BF16)
        return 0

    lax.fori_loop(0, inner * even, sum_a, 0)
    ga2 = [
        go(remote(ta.at[(i + k) % inner], ra2.at[k], ri_send.at[1, k], ri_recv.at[1, k], mate_in(k)))
        for k in range(1, inner)
    ]
    for copy in gb1:
        copy.wait_recv()

    def sum_b(s, _):
        oo, m = s // even, s % even
        total = sb1[oo, i, m].astype(F32)
        for k in range(1, inner):
            total += rb1[k, oo, m].astype(F32)
        tb[oo, m] = total.astype(BF16)
        return 0

    lax.fori_loop(0, outer * even, sum_b, 0)
    gb2 = [
        go(remote(tb.at[(o + k) % outer], rb2.at[k], ro_send.at[1, k], ro_recv.at[1, k], mate_out(k)))
        for k in range(1, outer)
    ]

    for copy in ga2 + gb2:
        copy.wait_recv()
    for m in range(even):
        total = ta[i, m].astype(F32)
        for k in range(1, inner):
            total += ra2[k, m].astype(F32)
        fin[m, parts[0]] = total.astype(BF16)
        total = tb[o, m].astype(F32)
        for k in range(1, outer):
            total += rb2[k, m].astype(F32)
        fin[m, parts[1]] = total.astype(BF16)
    for k in range(owners):
        d = (me + k) % owners
        start = 0
        for x in range(owners):
            start = start + jnp.where(x < d, counts_ref[x], 0)
        m = jnp.minimum(lax.div(start - me + owners - 1, owners), even - 1)
        if k == 0:
            grecv[me] = fin[m]
        else:
            gsend[k] = fin[m]
    x_copies = [
        go(remote(gsend.at[k], grecv.at[me], x_send.at[k], x_recv.at[k], mate(k)))
        for k in range(1, owners)
    ]

    for k, copy in enumerate(a2, 1):
        copy.wait_recv()
        place = held_ref.at[(o - k + outer) % outer, :, :, rows(0)]
        forward(place, place, fo_send.at[1, k], fo_recv.at[1, k])
    for k, copy in enumerate(b2, 1):
        copy.wait_recv()
        place = held_ref.at[:, (i - k + inner) % inner, :, rows(1)]
        forward(place, place, fi_send.at[1, k], fi_recv.at[1, k])

    for copy in x_copies:
        copy.wait_recv()
    for j in range(slots):
        used = jnp.where(j < my_count, 1.0, 0.0).astype(F32)
        block = grecv[lax.rem(my_off + j, owners)].astype(F32)
        out_ref[j, my_half] = (block * used).astype(BF16)
    place = out_ref.at[:, my_half]
    swap = remote(place, place, out_sems.at[0], out_sems.at[1], partner)
    swap.start()
    for copy in started:
        copy.wait_send()
    for copy in forwards:
        copy.wait()
    swap.wait()


def body(tokens, block_codes, scales, counts, cotangent):
    owners_total = lax.axis_size("fsdp")
    most_slots, tile = block_codes.shape[0], block_codes.shape[1]
    local_tokens, width = tokens.shape
    key_width = cotangent.shape[1]
    row_tiles, col_tiles = width // tile, key_width // tile
    block_count = row_tiles * col_tiles
    total_tokens = local_tokens * lax.axis_size("dp") * owners_total
    loss_scale = 1.0 / math.sqrt(total_tokens)
    inner = 4 if owners_total % 4 == 0 else 1
    outer = owners_total // inner
    even = block_count // owners_total
    half = tile // 2
    q0 = tile // 8
    q1 = half - q0
    assert even * owners_total == block_count and most_slots <= owners_total

    chunks = 8
    depth = width // chunks
    grads = pl.pallas_call(
        functools.partial(grad_kernel, loss_scale, tile),
        grid=(chunks,),
        in_specs=[
            pl.BlockSpec((local_tokens, depth), lambda g: (0, g)),
            pl.BlockSpec((local_tokens, key_width), lambda g: (0, 0)),
        ],
        out_specs=pl.BlockSpec((2, block_count // chunks, half, tile), lambda g: (0, g, 0, 0)),
        out_shape=jax.ShapeDtypeStruct((2, block_count, half, tile), BF16),
    )(tokens, cotangent)

    dma = pltpu.SemaphoreType.DMA
    vmem = pl.BlockSpec(memory_space=pltpu.VMEM)
    smem = pl.BlockSpec(memory_space=pltpu.SMEM)
    pairs_in, pairs_out = dma((2, inner)), dma((2, outer))
    held, block_grad = pl.pallas_call(
        functools.partial(comm_kernel, outer, inner, q0),
        in_specs=[smem, smem, vmem, vmem],
        out_specs=[pl.BlockSpec(memory_space=pl.ANY), vmem],
        out_shape=[
            jax.ShapeDtypeStruct((outer, inner, even, tile, tile), BF16),
            jax.ShapeDtypeStruct((most_slots, tile, tile), BF16),
        ],
        scratch_shapes=[
            pltpu.VMEM((block_count, half, tile), BF16),
            pltpu.VMEM((owners_total, half, tile), BF16),
            pltpu.VMEM((owners_total, half, tile), BF16),
            pltpu.VMEM((even, half, tile), BF16),
            pltpu.VMEM((outer, inner, even, q0, tile), BF16),
            pltpu.VMEM((outer, inner, even, q1, tile), BF16),
            pltpu.VMEM((outer, inner, even, q0, tile), BF16),
            pltpu.VMEM((inner, outer, even, q1, tile), BF16),
            pltpu.VMEM((inner, even, q0, tile), BF16),
            pltpu.VMEM((outer, even, q1, tile), BF16),
            pltpu.VMEM((inner, even, q0, tile), BF16),
            pltpu.VMEM((outer, even, q1, tile), BF16),
            pltpu.VMEM((even, half, tile), BF16),
            pltpu.VMEM((owners_total, half, tile), BF16),
            pltpu.VMEM((owners_total, half, tile), BF16),
            dma,
            dma((2,)),
            dma((owners_total,)), dma((owners_total,)), dma((owners_total,)), dma((owners_total,)),
            dma((2,)),
            pairs_in, pairs_in, pairs_out, pairs_out,
            pairs_in, pairs_in, pairs_out, pairs_out,
            pairs_in, pairs_in, pairs_out, pairs_out,
            dma((2,)),
        ],
        compiler_params=pltpu.CompilerParams(
            collective_id=0, has_side_effects=True, vmem_limit_bytes=48 * 1024 * 1024
        ),
    )(counts, scales, block_codes, grads)

    held = held.reshape(owners_total, even, tile, tile)
    projected, token_grad = pl.pallas_call(
        functools.partial(weight_kernel, tile, chunks, owners_total),
        grid_spec=pltpu.PrefetchScalarGridSpec(
            num_scalar_prefetch=0,
            grid=(chunks,),
            in_specs=[
                pl.BlockSpec((local_tokens, depth), lambda g: (0, g)),
                pl.BlockSpec((local_tokens, key_width), lambda g: (0, 0)),
                pl.BlockSpec(memory_space=pl.ANY),
            ],
            out_specs=[
                pl.BlockSpec((local_tokens, key_width), lambda g: (0, 0)),
                pl.BlockSpec((local_tokens, depth), lambda g: (0, g)),
            ],
            scratch_shapes=[
                pltpu.VMEM((chunks, depth, key_width), BF16),
                pltpu.VMEM((local_tokens, key_width), F32),
                dma((chunks,)),
            ],
        ),
        out_shape=[
            jax.ShapeDtypeStruct((local_tokens, key_width), BF16),
            jax.ShapeDtypeStruct((local_tokens, width), BF16),
        ],
    )(tokens, cotangent, held)

    return (projected, token_grad, block_grad)


def solution(mesh):
    return jax.shard_map(
        body,
        mesh=mesh,
        in_specs=(
            P(("dp", "fsdp"), None),
            P("fsdp", None, None),
            P("fsdp"),
            P(),
            P(("dp", "fsdp"), None),
        ),
        out_specs=(P(("dp", "fsdp"), None), P(("dp", "fsdp"), None), P("fsdp", None, None)),
        check_vma=False,
    )
```

time: 146 us -> 85.1 us (0.58)
  Pallas kernels: 137 us -> 81.2 us
  other arithmetic: 4.98 us -> 0 us
    pallas_call x2, Pallas kernels: 130 us -> 73.9 us  [the longest x1 65.3 us: body(): pl.pallas_call(functools.partial(comm_kernel, outer, inner, q0), in_specs...]
    reduce_sum x3 -> x0, other arithmetic: 1.47 us -> none  [the longest x1 1.29 us: body(): my_count = jnp.sum(jnp.where(is_mine, counts, 0))]
where the time goes in v2:
time: 85.1 us; the launch traced here: 84.6 us
  Pallas kernels  81.2 us (95%)
  local copies, waits for them, and re-layouts  2.73 us (3%)
    pallas_call x1, Pallas kernels, body(): pl.pallas_call(functools.partial(comm_kernel, outer, inner, q0), in_specs...  65.3 us
    pallas_call x1, Pallas kernels, body(): pl.pallas_call(functools.partial(weight_kernel, tile, chunks, owners_tota...  8.6 us
    pallas_call x1, Pallas kernels, body(): pl.pallas_call(functools.partial(grad_kernel, loss_scale, tile), grid=(ch...  7.29 us
    unnamed x9, local copies, waits for them, and re-layouts  2.73 us

profile of v2, /device:TPU:0, one launch (start us, length us, event | category | flops | bytes accessed | tf_op | source)
XLA Modules:
  0.0 84.6 jit_solution(3762297610997374745)
XLA Ops:
  0.6 0.0 copy-start.2
  0.6 0.0 copy-start.3
  0.7 0.0 copy-start.1
  0.7 7.3 %shard_map.76.g_ref = bf16[2,128,64,128]{3,2,1,0:T(8,128)(2,1)} custom-call(bf16[256,4096]{1,0:T(8,128)(2,1)} %tok_ref.3, bf16[256,512]{1,0:T(8,128)(2,1)} %cot_ref.3), custom_call_target="tpu_custom_call" | custom-call | tf_op jit(solution)/shard_map/pallas_call | solution.py:316
  8.0 0.0 copy-done.2
  8.0 0.0 copy-done.3
  8.0 0.0 copy-done.1
  8.0 65.3 %shard_map.77 = (bf16[4,4,8,128,128]{4,3,2,1,0:T(8,128)(2,1)S(1)}, bf16[16,128,128]{2,1,0:T(8,128)(2,1)S(1)}) custom-call(s32[16]{0:T(128)S(1)} %copy-done.2, f32[16]{0:T(128)S(1)} %copy-done.3, bf16[16,128,128]{2,1,0:T(8,128)(2,1)S(1)} %copy-done.1, bf16[2,128,64,128]{3,2,1,0:T(8,128)(2,1)} %shard_map.76.g_ref), custom_call_target="tpu_custom_call" | custom-call | tf_op jit(solution)/shard_map/pallas_call | solution.py:331
  73.3 0.0 copy-start
  73.3 1.9 %copy-done = bf16[4,4,8,128,128]{4,3,2,1,0:T(8,128)(2,1)} copy-done((bf16[4,4,8,128,128]{4,3,2,1,0:T(8,128)(2,1)}, bf16[4,4,8,128,128]{4,3,2,1,0:T(8,128)(2,1)S(1)}, u32[]{:S(2)}) %copy-start) | copy-done | bytes 4194328
  75.2 8.6 %shard_map.78 = (bf16[256,512]{1,0:T(8,128)(2,1)}, bf16[256,4096]{1,0:T(8,128)(2,1)}) custom-call(bf16[256,4096]{1,0:T(8,128)(2,1)} %tok_ref.3, bf16[256,512]{1,0:T(8,128)(2,1)} %cot_ref.3, bf16[16,8,128,128]{3,2,1,0:T(8,128)(2,1)} %bitcast.1), custom_call_target="tpu_custom_call" | custom-call | tf_op jit(solution)/shard_map/pallas_call | solution.py:370
  83.8 0.8 copy.9
Async XLA Ops:
  0.6 7.3 %copy-start.2 = (s32[16]{0:T(128)S(1)}, s32[16]{0:T(128)}, u32[]{:S(2)}) copy-start(s32[16]{0:T(128)} %counts_ref.1) | copy-start | bytes 196
  0.6 7.3 %copy-start.3 = (f32[16]{0:T(128)S(1)}, f32[16]{0:T(128)}, u32[]{:S(2)}) copy-start(f32[16]{0:T(128)} %scales_ref.1) | copy-start | bytes 196
  0.7 7.3 %copy-start.1 = (bf16[16,128,128]{2,1,0:T(8,128)(2,1)S(1)}, bf16[16,128,128]{2,1,0:T(8,128)(2,1)}, u32[]{:S(2)}) copy-start(bf16[16,128,128]{2,1,0:T(8,128)(2,1)} %codes_ref.1) | copy-start | bytes 1572868
  73.3 1.9 %copy-start = (bf16[4,4,8,128,128]{4,3,2,1,0:T(8,128)(2,1)}, bf16[4,4,8,128,128]{4,3,2,1,0:T(8,128)(2,1)S(1)}, u32[]{:S(2)}) copy-start(bf16[4,4,8,128,128]{4,3,2,1,0:T(8,128)(2,1)S(1)} %get-tuple-element.7) | copy-start | bytes 12582916

commit v3 on v2

--- a/solution.py
+++ b/solution.py
@@ -13,58 +13,10 @@
 BF16 = jnp.bfloat16
 
 
-def grad_kernel(scale, tile, tok_ref, cot_ref, out_ref):
-    half = tile // 2
-    part = lax.dot_general(
-        tok_ref[...], cot_ref[...], (((0,), (0,)), ((), ())), preferred_element_type=F32
-    )
-    part = (part * scale).astype(BF16)
-    rows, cols = part.shape[0] // tile, part.shape[1] // tile
-    for r in range(rows):
-        for c in range(cols):
-            for h in range(2):
-                top = r * tile + h * half
-                out_ref[h, r * cols + c] = part[top : top + half, c * tile : (c + 1) * tile]
-
-
-def weight_kernel(tile, chunks, owners, tok_ref, cot_ref, held_ref, proj_ref, tg_ref, w_ref, acc_ref, sems):
-    step = pl.program_id(0)
-    depth = w_ref.shape[1]
-    cols = w_ref.shape[2] // tile
-    rows = depth // tile
-
-    @pl.when(step == 0)
-    def _():
-        def fetch(g, _):
-            for r in range(rows):
-                for c in range(cols):
-                    b = (g * rows + r) * cols + c
-                    pltpu.make_async_copy(
-                        held_ref.at[b % owners, b // owners],
-                        w_ref.at[g, pl.ds(r * tile, tile), pl.ds(c * tile, tile)],
-                        sems.at[g],
-                    ).start()
-            return 0
-
-        lax.fori_loop(0, chunks, fetch, 0)
-        acc_ref[...] = jnp.zeros_like(acc_ref)
-
-    pltpu.make_async_copy(w_ref.at[step], w_ref.at[step], sems.at[step]).wait()
-    weight = w_ref[step]
-    acc_ref[...] += jnp.dot(tok_ref[...], weight, preferred_element_type=F32)
-    tg_ref[...] = lax.dot_general(
-        cot_ref[...], weight, (((1,), (1,)), ((), ())), preferred_element_type=F32
-    ).astype(BF16)
-
-    @pl.when(step == chunks - 1)
-    def _():
-        proj_ref[...] = acc_ref[...].astype(BF16)
-
-
 def comm_kernel(
-    outer, inner, q0, counts_ref, scales_ref, codes_ref, g_ref, held_ref, out_ref,
-    pair_buf, wsend, wrecv, stage, sb0, sb1, ra1, rb1, ta, tb, ra2, rb2, fin, gsend, grecv,
-    local_sem, pair_sems, w_send, w_recv, x_send, x_recv, own_sems,
+    outer, inner, q0, scale, counts_ref, scales_ref, codes_ref, tok_ref, cot_ref, proj_ref, tg_ref, out_ref,
+    g_ref, held_ref, w_ref, acc_ref, pair_buf, wsend, wrecv, stage, sb0, sb1, ra1, rb1, ta, tb, ra2, rb2, fin, gsend, grecv,
+    pair_sems, w_send, w_recv, x_send, x_recv, own_sems,
     gi_send, gi_recv, go_send, go_recv, fi_send, fi_recv, fo_send, fo_recv,
     ri_send, ri_recv, ro_send, ro_recv, out_sems,
 ):
@@ -114,8 +66,6 @@
         started.append(copy)
         return copy
 
-    pair = go(remote(g_ref.at[other], pair_buf, pair_sems.at[0], pair_sems.at[1], partner))
-
     offsets, ends, run, my_off, my_count = [], [], 0, 0, 0
     for d in range(owners):
         count = counts_ref[d]
@@ -138,6 +88,56 @@
         for k in range(1, owners)
     ]
 
+    depth = w_ref.shape[0]
+    chunks = tok_ref.shape[1] // depth
+    row_tiles, col_tiles = depth // tile, cot_ref.shape[1] // tile
+
+    def terms(g, _):
+        columns = pl.ds(pl.multiple_of(g * depth, depth), depth)
+        part = lax.dot_general(
+            tok_ref[:, columns], cot_ref[...], (((0,), (0,)), ((), ())), preferred_element_type=F32
+        )
+        part = (part * scale).astype(BF16)
+        for r in range(row_tiles):
+            for c in range(col_tiles):
+                for h in range(2):
+                    top = r * tile + h * half
+                    g_ref[h, (g * row_tiles + r) * col_tiles + c] = part[
+                        top : top + half, c * tile : (c + 1) * tile
+                    ]
+        return 0
+
+    lax.fori_loop(0, chunks, terms, 0)
+    pair = go(remote(g_ref.at[other], pair_buf, pair_sems.at[0], pair_sems.at[1], partner))
+
+    for copy in w_copies:
+        copy.wait_recv()
+    for m in range(even):
+        owner = 0
+        for d in range(owners):
+            owner = owner + jnp.where(ends[d] <= m * owners + me, 1, 0)
+        block = wrecv[jnp.minimum(owner, owners - 1)]
+        stage[m] = block
+        held_ref[o, i, m, my_half] = block
+    a1 = [
+        go(remote(stage.at[:, parts[0]], held_ref.at[o, i, :, rows(0)],
+                  gi_send.at[0, k], gi_recv.at[0, k], mate_in(k)))
+        for k in range(1, inner)
+    ]
+    b1 = [
+        go(remote(stage.at[:, parts[1]], held_ref.at[o, i, :, rows(1)],
+                  go_send.at[0, k], go_recv.at[0, k], mate_out(k)))
+        for k in range(1, outer)
+    ]
+    forwards = []
+
+    def forward(src, place, send, recv):
+        copy = remote(src, place, send, recv, partner)
+        copy.start()
+        forwards.append(copy)
+
+    forward(stage, held_ref.at[o, i, :, my_half], own_sems.at[0], own_sems.at[1])
+
     pair.wait_recv()
 
     def build(s, _):
@@ -160,35 +160,6 @@
         for k in range(1, inner)
     ]
 
-    for copy in w_copies:
-        copy.wait_recv()
-    for m in range(even):
-        owner = 0
-        for d in range(owners):
-            owner = owner + jnp.where(ends[d] <= m * owners + me, 1, 0)
-        stage[m] = wrecv[jnp.minimum(owner, owners - 1)]
-    a1 = [
-        go(remote(stage.at[:, parts[0]], held_ref.at[o, i, :, rows(0)],
-                  gi_send.at[0, k], gi_recv.at[0, k], mate_in(k)))
-        for k in range(1, inner)
-    ]
-    b1 = [
-        go(remote(stage.at[:, parts[1]], held_ref.at[o, i, :, rows(1)],
-                  go_send.at[0, k], go_recv.at[0, k], mate_out(k)))
-        for k in range(1, outer)
-    ]
-    mine = pltpu.make_async_copy(stage, held_ref.at[o, i, :, my_half], local_sem)
-    mine.start()
-    forwards = []
-
-    def forward(src, place, send, recv):
-        copy = remote(src, place, send, recv, partner)
-        copy.start()
-        forwards.append(copy)
-
-    forward(stage, held_ref.at[o, i, :, my_half], own_sems.at[0], own_sems.at[1])
-
-    mine.wait()
     for copy in a1:
         copy.wait_recv()
     a2 = [
@@ -242,6 +213,15 @@
         go(remote(tb.at[(o + k) % outer], rb2.at[k], ro_send.at[1, k], ro_recv.at[1, k], mate_out(k)))
         for k in range(1, outer)
     ]
+
+    for k, copy in enumerate(a2, 1):
+        copy.wait_recv()
+        place = held_ref.at[(o - k + outer) % outer, :, :, rows(0)]
+        forward(place, place, fo_send.at[1, k], fo_recv.at[1, k])
+    for k, copy in enumerate(b2, 1):
+        copy.wait_recv()
+        place = held_ref.at[:, (i - k + inner) % inner, :, rows(1)]
+        forward(place, place, fi_send.at[1, k], fi_recv.at[1, k])
 
     for copy in ga2 + gb2:
         copy.wait_recv()
@@ -269,14 +249,26 @@
         for k in range(1, owners)
     ]
 
-    for k, copy in enumerate(a2, 1):
-        copy.wait_recv()
-        place = held_ref.at[(o - k + outer) % outer, :, :, rows(0)]
-        forward(place, place, fo_send.at[1, k], fo_recv.at[1, k])
-    for k, copy in enumerate(b2, 1):
-        copy.wait_recv()
-        place = held_ref.at[:, (i - k + inner) % inner, :, rows(1)]
-        forward(place, place, fi_send.at[1, k], fi_recv.at[1, k])
+    for copy in forwards:
+        copy.wait_recv()
+    acc_ref[...] = jnp.zeros_like(acc_ref)
+
+    def products(g, _):
+        columns = pl.ds(pl.multiple_of(g * depth, depth), depth)
+        for r in range(row_tiles):
+            for c in range(col_tiles):
+                b = (g * row_tiles + r) * col_tiles + c
+                e, m = b % owners, b // owners
+                w_ref[r * tile : (r + 1) * tile, c * tile : (c + 1) * tile] = held_ref[e // inner, e % inner, m]
+        weight = w_ref[...]
+        acc_ref[...] += jnp.dot(tok_ref[:, columns], weight, preferred_element_type=F32)
+        tg_ref[:, columns] = lax.dot_general(
+            cot_ref[...], weight, (((1,), (1,)), ((), ())), preferred_element_type=F32
+        ).astype(BF16)
+        return 0
+
+    lax.fori_loop(0, chunks, products, 0)
+    proj_ref[...] = acc_ref[...].astype(BF16)
 
     for copy in x_copies:
         copy.wait_recv()
@@ -290,7 +282,7 @@
     for copy in started:
         copy.wait_send()
     for copy in forwards:
-        copy.wait()
+        copy.wait_send()
     swap.wait()
 
 
@@ -313,30 +305,24 @@
 
     chunks = 8
     depth = width // chunks
-    grads = pl.pallas_call(
-        functools.partial(grad_kernel, loss_scale, tile),
-        grid=(chunks,),
-        in_specs=[
-            pl.BlockSpec((local_tokens, depth), lambda g: (0, g)),
-            pl.BlockSpec((local_tokens, key_width), lambda g: (0, 0)),
-        ],
-        out_specs=pl.BlockSpec((2, block_count // chunks, half, tile), lambda g: (0, g, 0, 0)),
-        out_shape=jax.ShapeDtypeStruct((2, block_count, half, tile), BF16),
-    )(tokens, cotangent)
-
     dma = pltpu.SemaphoreType.DMA
     vmem = pl.BlockSpec(memory_space=pltpu.VMEM)
     smem = pl.BlockSpec(memory_space=pltpu.SMEM)
     pairs_in, pairs_out = dma((2, inner)), dma((2, outer))
-    held, block_grad = pl.pallas_call(
-        functools.partial(comm_kernel, outer, inner, q0),
-        in_specs=[smem, smem, vmem, vmem],
-        out_specs=[pl.BlockSpec(memory_space=pl.ANY), vmem],
+    return tuple(pl.pallas_call(
+        functools.partial(comm_kernel, outer, inner, q0, loss_scale),
+        in_specs=[smem, smem, vmem, vmem, vmem],
+        out_specs=[vmem, vmem, vmem],
         out_shape=[
-            jax.ShapeDtypeStruct((outer, inner, even, tile, tile), BF16),
+            jax.ShapeDtypeStruct((local_tokens, key_width), BF16),
+            jax.ShapeDtypeStruct((local_tokens, width), BF16),
             jax.ShapeDtypeStruct((most_slots, tile, tile), BF16),
         ],
         scratch_shapes=[
+            pltpu.VMEM((2, block_count, half, tile), BF16),
+            pltpu.VMEM((outer, inner, even, tile, tile), BF16),
+            pltpu.VMEM((depth, key_width), BF16),
+            pltpu.VMEM((local_tokens, key_width), F32),
             pltpu.VMEM((block_count, half, tile), BF16),
             pltpu.VMEM((owners_total, half, tile), BF16),
             pltpu.VMEM((owners_total, half, tile), BF16),
@@ -352,7 +338,6 @@
             pltpu.VMEM((even, half, tile), BF16),
             pltpu.VMEM((owners_total, half, tile), BF16),
             pltpu.VMEM((owners_total, half, tile), BF16),
-            dma,
             dma((2,)),
             dma((owners_total,)), dma((owners_total,)), dma((owners_total,)), dma((owners_total,)),
             dma((2,)),
@@ -364,36 +349,7 @@
         compiler_params=pltpu.CompilerParams(
             collective_id=0, has_side_effects=True, vmem_limit_bytes=48 * 1024 * 1024
         ),
-    )(counts, scales, block_codes, grads)
-
-    held = held.reshape(owners_total, even, tile, tile)
-    projected, token_grad = pl.pallas_call(
-        functools.partial(weight_kernel, tile, chunks, owners_total),
-        grid_spec=pltpu.PrefetchScalarGridSpec(
-            num_scalar_prefetch=0,
-            grid=(chunks,),
-            in_specs=[
-                pl.BlockSpec((local_tokens, depth), lambda g: (0, g)),
-                pl.BlockSpec((local_tokens, key_width), lambda g: (0, 0)),
-                pl.BlockSpec(memory_space=pl.ANY),
-            ],
-            out_specs=[
-                pl.BlockSpec((local_tokens, key_width), lambda g: (0, 0)),
-                pl.BlockSpec((local_tokens, depth), lambda g: (0, g)),
-            ],
-            scratch_shapes=[
-                pltpu.VMEM((chunks, depth, key_width), BF16),
-                pltpu.VMEM((local_tokens, key_width), F32),
-                dma((chunks,)),
-            ],
-        ),
-        out_shape=[
-            jax.ShapeDtypeStruct((local_tokens, key_width), BF16),
-            jax.ShapeDtypeStruct((local_tokens, width), BF16),
-        ],
-    )(tokens, cotangent, held)
-
-    return (projected, token_grad, block_grad)
+    )(counts, scales, block_codes, tokens, cotangent))
 
 
 def solution(mesh):

time: 85.1 us -> 73.1 us (0.86)
  Pallas kernels: 81.2 us -> 64.5 us
  local copies, waits for them, and re-layouts: 2.73 us -> 7.7 us
    pallas_call x3 -> x1, Pallas kernels: 81.2 us -> 64.5 us  [body(): pl.pallas_call(functools.partial(comm_kernel, outer, inner, q0, loss_scal...]
    unnamed x9 -> x13, local copies, waits for them, and re-layouts: 2.73 us -> 7.7 us
where the time goes in v3:
time: 73.1 us; the launch traced here: 72.9 us
  Pallas kernels  64.5 us (88%)
  local copies, waits for them, and re-layouts  7.7 us (11%)
    pallas_call x1, Pallas kernels, body(): pl.pallas_call(functools.partial(comm_kernel, outer, inner, q0, loss_scal...  64.5 us
    unnamed x13, local copies, waits for them, and re-layouts  7.7 us

profile of v3, /device:TPU:0, one launch (start us, length us, event | category | flops | bytes accessed | tf_op | source)
XLA Modules:
  0.0 72.9 jit_solution(7106069540832638963)
XLA Ops:
  0.6 0.0 copy-start
  0.6 1.6 %copy-done = bf16[256,4096]{1,0:T(8,128)(2,1)S(1)} copy-done((bf16[256,4096]{1,0:T(8,128)(2,1)S(1)}, bf16[256,4096]{1,0:T(8,128)(2,1)}, u32[]{:S(2)}) %copy-start) | copy-done | bytes 2097176
  2.2 0.0 copy-start.1
  2.2 1.0 %copy-done.1 = bf16[16,128,128]{2,1,0:T(8,128)(2,1)S(1)} copy-done((bf16[16,128,128]{2,1,0:T(8,128)(2,1)S(1)}, bf16[16,128,128]{2,1,0:T(8,128)(2,1)}, u32[]{:S(2)}) %copy-start.1) | copy-done | bytes 524312
  3.3 0.0 copy-start.2
  3.3 0.9 %copy-done.2 = bf16[256,512]{1,0:T(8,128)(2,1)S(1)} copy-done((bf16[256,512]{1,0:T(8,128)(2,1)S(1)}, bf16[256,512]{1,0:T(8,128)(2,1)}, u32[]{:S(2)}) %copy-start.2) | copy-done | bytes 262168
  4.2 0.0 copy-start.3
  4.2 0.7 copy-done.3
  4.9 0.0 copy-start.4
  4.9 0.7 copy-done.4
  5.5 64.5 %shard_map.76 = (bf16[256,512]{1,0:T(8,128)(2,1)S(1)}, bf16[256,4096]{1,0:T(8,128)(2,1)S(1)}, bf16[16,128,128]{2,1,0:T(8,128)(2,1)S(1)}) custom-call(s32[16]{0:T(128)S(1)} %copy-done.3, f32[16]{0:T(128)S(1)} %copy-done.4, bf16[16,128,128]{2,1,0:T(8,128)(2,1)S(1)} %copy-done.1, bf16[256,4096]{1,0:T(8,128)(2,1)S(1)} %copy-done, bf16[256,512]{1,0:T(8,128)(2,1)S(1)} %copy-done.2), custom_call_target="tpu_custom_call" | custom-call | tf_op jit(solution)/shard_map/pallas_call | solution.py:312
  70.0 0.7 copy.11
  70.7 1.3 %copy.12 = bf16[256,4096]{1,0:T(8,128)(2,1)} copy(bf16[256,4096]{1,0:T(8,128)(2,1)S(1)} %get-tuple-element.7) | data formatting | bytes 4194304
  72.1 0.8 %copy.13 = bf16[16,128,128]{2,1,0:T(8,128)(2,1)} copy(bf16[16,128,128]{2,1,0:T(8,128)(2,1)S(1)} %get-tuple-element.8) | data formatting | bytes 1048576
Async XLA Ops:
  0.6 1.6 %copy-start = (bf16[256,4096]{1,0:T(8,128)(2,1)S(1)}, bf16[256,4096]{1,0:T(8,128)(2,1)}, u32[]{:S(2)}) copy-start(bf16[256,4096]{1,0:T(8,128)(2,1)} %tok_ref.1) | copy-start | bytes 6291460
  2.2 1.0 %copy-start.1 = (bf16[16,128,128]{2,1,0:T(8,128)(2,1)S(1)}, bf16[16,128,128]{2,1,0:T(8,128)(2,1)}, u32[]{:S(2)}) copy-start(bf16[16,128,128]{2,1,0:T(8,128)(2,1)} %codes_ref.1) | copy-start | bytes 1572868
  3.3 0.9 %copy-start.2 = (bf16[256,512]{1,0:T(8,128)(2,1)S(1)}, bf16[256,512]{1,0:T(8,128)(2,1)}, u32[]{:S(2)}) copy-start(bf16[256,512]{1,0:T(8,128)(2,1)} %cot_ref.1) | copy-start | bytes 786436
  4.2 0.7 copy-start.3
  4.9 0.7 copy-start.4
